TPU v7x, 32 devices: a whole 2x2x4 slice. The times are simulated.
32 devices in a mesh: lat: 4 (over y, x), lon: 8 (over z, core).
Axes of the slice: x: 2, y: 2, z: 4, core: 2. Of those that a mesh axis runs over, the one named last changes fastest.
Arguments:
- forcing: float32 [256, 2048], P('lat', 'lon'), may hold values from -32 to 32
- depth_east: float32 [256, 2048], P('lat', 'lon'), may hold values from 0.25 to 4
- depth_north: float32 [256, 2048], P('lat', 'lon'), may hold values from 0.25 to 4
- surface_term: float32 [256, 2048], P('lat', 'lon'), may hold values from 0.02 to 0.5
- ocean_mask: int32 [256, 2048], P('lat', 'lon'), may hold values 0 or 1
- cost_weights: float32 [8, 256, 2048], P(None, 'lat', 'lon'), may hold values from -6 to 6
Outputs:
- forcing_adjoint: float32 [8, 256, 2048], P(None, 'lat', 'lon')
- east_gradient: float32 [8, 256, 2048], P(None, 'lat', 'lon')
- north_gradient: float32 [8, 256, 2048], P(None, 'lat', 'lon')
Inputs may be any that keep to these rules, and one draw needn't show every extreme that they name: `ocean_mask`: 1 marks an ocean cell, 0 a land cell.
All inputs are finite; a program needn't handle non-finite values. No bound on the sum of `ocean_mask` on one device may be relied on, other than what follows from the above.
Results may differ from a plain program's by a relative error of at most 0.00018.
Values sent between devices are 32-bit elements; how exact they have to be, the bound alone decides.
A program may use at most 64 MiB of HBM per device.

v0:
```python
import jax
import jax.numpy as jnp
from jax import lax
from jax.sharding import PartitionSpec as P

ITERS = 6


def padded_2(block, sides, width, periodic):
    for axis, dim in sides:
        count = lax.axis_size(axis)
        forward = [(i, i + 1) for i in range(count - 1)]
        if periodic:
            forward.append((count - 1, 0))
        backward = [(target, source) for source, target in forward]
        low = lax.ppermute(
            lax.slice_in_dim(block, block.shape[dim] - width, None, axis=dim), axis, forward
        )
        high = lax.ppermute(lax.slice_in_dim(block, 0, width, axis=dim), axis, backward)
        block = jnp.concatenate([low, block, high], axis=dim)
    return block


def shifted(value, axis, steps):
    count = lax.axis_size(axis)
    pairs = [(source, (source + steps) % count) for source in range(count)]
    return lax.ppermute(value, axis, pairs)


def shifted_2(block, axis, distance):
    devices = range(lax.axis_size(axis))
    route = [(i - distance, i) for i in devices if i - distance in devices]
    return lax.ppermute(block, axis, route)


def widen_coefs(stacked):
    wider = padded_2(stacked, (("lon", 2),), 1, True)
    return padded_2(wider, (("lat", 1),), 1, False)


def widen_precond(field):
    wider = padded_2(field, (("lon", 1),), 1, True)
    return padded_2(wider, (("lat", 0),), 1, False)


def widen_image(stack):
    wider = padded_2(stack, (("lon", 2),), 1, True)
    return padded_2(wider, (("lat", 1),), 1, False)


def operate(padded, coefs):
    base, east_face, west_face, north_face, south_face = coefs
    centre = padded[..., 1:-1, 1:-1]
    return (
        base * centre
        + east_face * (centre - padded[..., 1:-1, 2:])
        + west_face * (centre - padded[..., 1:-1, :-2])
        + north_face * (centre - padded[..., 2:, 1:-1])
        + south_face * (centre - padded[..., :-2, 1:-1])
    )


def smoothed_terms(residual, diagonal, coefs):
    precond = residual / diagonal
    prec_pad = widen_precond(precond)
    smooth = operate(prec_pad, coefs)
    norm_value, delta = lax.psum(
        (jnp.sum(residual * precond), jnp.sum(precond * smooth)), ("lat", "lon")
    )
    return (prec_pad, smooth, norm_value, delta)


def body(forcing, depth_east, depth_north, surface_term, ocean_mask, cost_weights):
    stacked = jnp.stack([ocean_mask.astype(jnp.float32), depth_east, depth_north])
    padded = widen_coefs(stacked)
    wet = padded[0]
    east_all = padded[1][:, :-1] * wet[:, :-1] * wet[:, 1:]
    north_all = padded[2][:-1, :] * wet[:-1, :] * wet[1:, :]
    east_face = east_all[1:-1, 1:]
    west_face = east_all[1:-1, :-1]
    north_face = north_all[1:, 1:-1]
    south_face = north_all[:-1, 1:-1]
    ocean = wet[1:-1, 1:-1]
    mask_east = ocean * wet[1:-1, 2:]
    mask_north = ocean * wet[2:, 1:-1]
    base = ocean * surface_term + 1.0 - ocean
    diagonal = base + east_face + west_face + north_face + south_face
    coefs = (base, east_face, west_face, north_face, south_face)
    residual = forcing
    padded_dirs = []
    images = []
    residuals = []
    alphas = []
    betas = []
    pairs = []
    prec_pad, smooth, norm_first, delta = smoothed_terms(residual, diagonal, coefs)
    norms = [norm_first]
    alpha = norm_first / delta
    dir_pad = prec_pad
    image = smooth
    for step in range(ITERS):
        padded_dirs.append(dir_pad)
        images.append(image)
        alphas.append(alpha)
        pairs.append(norms[-1] / alpha)
        residual = residual - alpha * image
        if step < ITERS - 1:
            residuals.append(residual)
            prec_pad, smooth, norm_next, delta = smoothed_terms(residual, diagonal, coefs)
            beta = norm_next / norms[-1]
            alpha = norm_next / (delta - beta * norm_next / alpha)
            dir_pad = prec_pad + beta * dir_pad
            image = smooth + beta * image
            norms.append(norm_next)
            betas.append(beta)
    projections = lax.psum(
        jnp.stack(
            [
                jnp.sum(cost_weights * padded_dirs[step][1:-1, 1:-1], axis=(1, 2))
                for step in range(ITERS)
            ]
        ),
        ("lat", "lon"),
    )
    last = ITERS - 1
    dir_pad = padded_dirs[last]
    inner_dir = dir_pad[1:-1, 1:-1]
    alpha_bar = projections[last]
    norm_bar = alpha_bar / pairs[last]
    pair_bar = -alpha_bar * alphas[last] / pairs[last]
    scale = pair_bar[:, None, None]
    dir_bar = alphas[last] * cost_weights + 2.0 * scale * images[last]
    east_diff = inner_dir - dir_pad[1:-1, 2:]
    north_diff = inner_dir - dir_pad[2:, 1:-1]
    east_sum = scale * (east_diff * east_diff)
    north_sum = scale * (north_diff * north_diff)
    res_bar = jnp.zeros_like(cost_weights)
    depth_bar = jnp.zeros_like(cost_weights)
    for step in range(ITERS - 2, -1, -1):
        dir_pad = padded_dirs[step]
        inner_dir = dir_pad[1:-1, 1:-1]
        image = images[step]
        resid_next = residuals[step]
        precond_next = resid_next / diagonal
        scaled = dir_bar / diagonal
        beta_term = lax.psum(jnp.sum(dir_bar * inner_dir, axis=(1, 2)), ("lat", "lon"))
        norm_next_bar = norm_bar + beta_term / norms[step]
        res_new = res_bar + scaled + 2.0 * norm_next_bar[:, None, None] * precond_next
        alpha_bar = projections[step] - lax.psum(
            jnp.sum(res_new * image, axis=(1, 2)), ("lat", "lon")
        )
        pre_bar = dir_bar + norm_next_bar[:, None, None] * resid_next
        depth_bar = depth_bar - pre_bar * precond_next / diagonal
        norm_bar = (
            -beta_term * norms[step + 1] / (norms[step] * norms[step]) + alpha_bar / pairs[step]
        )
        pair_bar = -alpha_bar * alphas[step] / pairs[step]
        scale = pair_bar[:, None, None]
        image_pad = widen_image(-alphas[step] * res_new + scale * inner_dir)
        dir_bar = (
            betas[step] * dir_bar
            + alphas[step] * cost_weights
            + scale * image
            + operate(image_pad, coefs)
        )
        centre = image_pad[:, 1:-1, 1:-1]
        east_sum = east_sum + (centre - image_pad[:, 1:-1, 2:]) * (inner_dir - dir_pad[1:-1, 2:])
        north_sum = north_sum + (centre - image_pad[:, 2:, 1:-1]) * (inner_dir - dir_pad[2:, 1:-1])
        res_bar = res_new
    precond_first = forcing / diagonal
    pre_bar = dir_bar + norm_bar[:, None, None] * forcing
    forcing_adjoint = res_bar + dir_bar / diagonal + 2.0 * norm_bar[:, None, None] * precond_first
    depth_bar = depth_bar - pre_bar * precond_first / diagonal
    east_column = shifted(depth_bar[:, :, :1], "lon", -1)
    north_row = shifted_2(depth_bar[:, :1, :], "lat", -1)
    depth_eastward = jnp.concatenate([depth_bar[:, :, 1:], east_column], axis=2)
    depth_northward = jnp.concatenate([depth_bar[:, 1:, :], north_row], axis=1)
    east_gradient = mask_east * (east_sum + depth_bar + depth_eastward)
    north_gradient = mask_north * (north_sum + depth_bar + depth_northward)
    return (forcing_adjoint, east_gradient, north_gradient)


def solution(mesh):
    return jax.shard_map(
        body,
        mesh=mesh,
        in_specs=(
            P("lat", "lon"),
            P("lat", "lon"),
            P("lat", "lon"),
            P("lat", "lon"),
            P("lat", "lon"),
            P(None, "lat", "lon"),
        ),
        out_specs=(P(None, "lat", "lon"), P(None, "lat", "lon"), P(None, "lat", "lon")),
        check_vma=False,
    )
```

profile of v0, /device:TPU:0, one launch (start us, length us, event | category | flops | bytes accessed | tf_op | source)
XLA Modules:
  0.0 976.1 jit_solution(14568244211439639987)
XLA Ops:
  28.7 4.9 collective-permute-start.7
  35.7 39.7 %all-reduce.5 = (f32[]{:T(128)}, f32[]{:T(128)}) all-reduce(f32[]{:T(128)} %get-tuple-element.20, f32[]{:T(128)} %get-tuple-element.19), channel_id=1, replica_groups=mesh['lat'=4,'lon'=8] {'lat','lon'}, use_global_device_ids=true, to_apply=%region_1.0 | all-reduce | flops 2 | bytes 16 | tf_op jit(solution)/shard_map/psum | solution.py:67
  84.7 5.3 collective-permute-start.11
  92.0 40.0 %all-reduce.4 = (f32[]{:T(128)}, f32[]{:T(128)}) all-reduce(f32[]{:T(128)} %get-tuple-element.18, f32[]{:T(128)} %get-tuple-element.17), channel_id=1, replica_groups=mesh['lat'=4,'lon'=8] {'lat','lon'}, use_global_device_ids=true, to_apply=%region_5.0 | all-reduce | flops 2 | bytes 16 | tf_op jit(solution)/shard_map/psum | solution.py:67
  144.4 5.3 collective-permute-start.15
  151.7 39.8 %all-reduce.3 = (f32[]{:T(128)}, f32[]{:T(128)}) all-reduce(f32[]{:T(128)} %get-tuple-element.16, f32[]{:T(128)} %get-tuple-element.15), channel_id=1, replica_groups=mesh['lat'=4,'lon'=8] {'lat','lon'}, use_global_device_ids=true, to_apply=%region_9.0 | all-reduce | flops 2 | bytes 16 | tf_op jit(solution)/shard_map/psum | solution.py:67
  203.2 5.3 collective-permute-start.19
  210.5 40.0 %all-reduce.2 = (f32[]{:T(128)}, f32[]{:T(128)}) all-reduce(f32[]{:T(128)} %get-tuple-element.14, f32[]{:T(128)} %get-tuple-element.13), channel_id=1, replica_groups=mesh['lat'=4,'lon'=8] {'lat','lon'}, use_global_device_ids=true, to_apply=%region_13.0 | all-reduce | flops 2 | bytes 16 | tf_op jit(solution)/shard_map/psum | solution.py:67
  262.0 5.3 collective-permute-start.23
  269.4 39.8 %all-reduce.1 = (f32[]{:T(128)}, f32[]{:T(128)}) all-reduce(f32[]{:T(128)} %get-tuple-element.12, f32[]{:T(128)} %get-tuple-element.11), channel_id=1, replica_groups=mesh['lat'=4,'lon'=8] {'lat','lon'}, use_global_device_ids=true, to_apply=%region_17.0 | all-reduce | flops 2 | bytes 16 | tf_op jit(solution)/shard_map/psum | solution.py:67
  320.6 5.3 collective-permute-start.27
  327.9 40.0 %psum.171 = f32[]{:T(128)} all-reduce(f32[]{:T(128)} %get-tuple-element.10), channel_id=1, replica_groups=mesh['lat'=4,'lon'=8] {'lat','lon'}, use_global_device_ids=true, to_apply=%region_21.0 | all-reduce | flops 1 | bytes 8 | tf_op jit(solution)/shard_map/psum | solution.py:67
  374.1 42.9 %all-reduce = (f32[6,8]{1,0:T(8,128)S(1)}, f32[]{:T(128)}) all-reduce(f32[6,8]{1,0:T(8,128)S(1)} %stack.43, f32[]{:T(128)} %get-tuple-element.9), channel_id=1, replica_groups=mesh['lat'=4,'lon'=8] {'lat','lon'}, use_global_device_ids=true, to_apply=%region_30.0 | all-reduce | flops 49 | bytes 392 | tf_op jit(solution)/shard_map/psum | solution.py:116
  421.1 38.5 %psum.174 = f32[8]{0:T(128)S(1)} all-reduce(f32[8]{0:T(128)S(1)} %multiply_reduce_fusion.9), channel_id=1, replica_groups=mesh['lat'=4,'lon'=8] {'lat','lon'}, use_global_device_ids=true, to_apply=%region_32.0 | all-reduce | flops 8 | bytes 64 | tf_op jit(solution)/shard_map/psum | solution.py:146
  461.0 41.8 %psum.175 = f32[8]{0:T(128)S(1)} all-reduce(f32[8]{0:T(128)S(1)} %get-tuple-element.61), channel_id=1, replica_groups=mesh['lat'=4,'lon'=8] {'lat','lon'}, use_global_device_ids=true, to_apply=%region_34.0 | all-reduce | flops 8 | bytes 64 | tf_op jit(solution)/shard_map/psum | solution.py:149
  504.7 6.3 collective-permute-done.28
  525.7 39.5 %psum.176 = f32[8]{0:T(128)S(1)} all-reduce(f32[8]{0:T(128)S(1)} %copy-done.108), channel_id=1, replica_groups=mesh['lat'=4,'lon'=8] {'lat','lon'}, use_global_device_ids=true, to_apply=%region_36.0 | all-reduce | flops 8 | bytes 64 | tf_op jit(solution)/shard_map/psum | solution.py:146
  568.0 41.8 %psum.177 = f32[8]{0:T(128)S(1)} all-reduce(f32[8]{0:T(128)S(1)} %get-tuple-element.55), channel_id=1, replica_groups=mesh['lat'=4,'lon'=8] {'lat','lon'}, use_global_device_ids=true, to_apply=%region_38.0 | all-reduce | flops 8 | bytes 64 | tf_op jit(solution)/shard_map/psum | solution.py:149
  611.8 6.3 collective-permute-done.32
  622.0 5.4 collective-permute-start.35
  633.2 38.5 %psum.178 = f32[8]{0:T(128)} all-reduce(f32[8]{0:T(128)} %get-tuple-element.53), channel_id=1, replica_groups=mesh['lat'=4,'lon'=8] {'lat','lon'}, use_global_device_ids=true, to_apply=%region_40.0 | all-reduce | flops 8 | bytes 64 | tf_op jit(solution)/shard_map/psum | solution.py:146
  677.1 42.0 %psum.179 = f32[8]{0:T(128)S(1)} all-reduce(f32[8]{0:T(128)S(1)} %copy-done.107), channel_id=1, replica_groups=mesh['lat'=4,'lon'=8] {'lat','lon'}, use_global_device_ids=true, to_apply=%region_42.0 | all-reduce | flops 8 | bytes 64 | tf_op jit(solution)/shard_map/psum | solution.py:149
  722.2 6.3 collective-permute-done.36
  732.4 5.4 collective-permute-start.39
  744.6 39.2 %psum.180 = f32[8]{0:T(128)S(1)} all-reduce(f32[8]{0:T(128)S(1)} %copy-done.109), channel_id=1, replica_groups=mesh['lat'=4,'lon'=8] {'lat','lon'}, use_global_device_ids=true, to_apply=%region_44.0 | all-reduce | flops 8 | bytes 64 | tf_op jit(solution)/shard_map/psum | solution.py:146
  788.3 41.5 %psum.181 = f32[8]{0:T(128)S(1)} all-reduce(f32[8]{0:T(128)S(1)} %get-tuple-element.43), channel_id=1, replica_groups=mesh['lat'=4,'lon'=8] {'lat','lon'}, use_global_device_ids=true, to_apply=%region_46.0 | all-reduce | flops 8 | bytes 64 | tf_op jit(solution)/shard_map/psum | solution.py:149
  832.9 6.3 collective-permute-done.40
  843.1 5.6 collective-permute-start.43
  856.8 38.4 %psum.182 = f32[8]{0:T(128)} all-reduce(f32[8]{0:T(128)} %get-tuple-element.41), channel_id=1, replica_groups=mesh['lat'=4,'lon'=8] {'lat','lon'}, use_global_device_ids=true, to_apply=%region_48.0 | all-reduce | flops 8 | bytes 64 | tf_op jit(solution)/shard_map/psum | solution.py:146
  900.4 42.1 %psum.183 = f32[8]{0:T(128)} all-reduce(f32[8]{0:T(128)} %get-tuple-element.37), channel_id=1, replica_groups=mesh['lat'=4,'lon'=8] {'lat','lon'}, use_global_device_ids=true, to_apply=%region_50.0 | all-reduce | flops 8 | bytes 64 | tf_op jit(solution)/shard_map/psum | solution.py:149
  945.9 6.5 collective-permute-done.44
  955.6 4.9 collective-permute-start.47
  (388 shorter events, 169.0 us)
Async XLA Ops:
  1.7 6.9 collective-permute-start
  2.2 6.4 collective-permute-start.1
  83.4 6.6 collective-permute-start.10
  84.7 6.5 collective-permute-start.11
  143.1 6.6 collective-permute-start.14
  144.4 6.5 collective-permute-start.15
  201.9 6.6 collective-permute-start.18
  203.2 6.5 collective-permute-start.19
  260.7 6.6 collective-permute-start.22
  262.0 6.5 collective-permute-start.23
  319.3 7.1 collective-permute-start.26
  320.6 6.5 collective-permute-start.27
  504.2 6.8 collective-permute-start.28
  504.4 8.5 collective-permute-start.29
  513.1 8.5 collective-permute-start.30
  514.4 7.2 collective-permute-start.31
  611.2 6.8 collective-permute-start.32
  611.5 8.5 collective-permute-start.33
  620.7 9.2 collective-permute-start.34
  622.0 8.5 collective-permute-start.35
  721.6 6.8 collective-permute-start.36
  721.9 8.5 collective-permute-start.37
  731.1 9.2 collective-permute-start.38
  732.4 7.9 collective-permute-start.39
  832.3 6.8 collective-permute-start.40
  832.6 8.5 collective-permute-start.41
  841.9 11.4 %collective-permute-start.42 = (f32[8,1,258]{2,1,0:T(1,128)}, f32[8,1,258]{2,1,0:T(1,128)}, u32[]{:S(2)}, u32[]{:S(2)}) collective-permute-start(f32[8,1,258]{2,1,0:T(1,128)} %get-tuple-element.97), channel_id=1, source_target_pairs={{8,0},{16,8},{24,16},{9,1},{17,9},{25,17},{10,2},{18,10},{26,18},{... | collective-permute-start | bytes 24776 | tf_op jit(solution)/shard_map/ppermute | solution.py:19
  843.1 10.1 %collective-permute-start.43 = (f32[8,1,258]{2,1,0:T(1,128)}, f32[8,1,258]{2,1,0:T(1,128)}, u32[]{:S(2)}, u32[]{:S(2)}) collective-permute-start(f32[8,1,258]{2,1,0:T(1,128)} %get-tuple-element.98), channel_id=1, source_target_pairs={{0,8},{8,16},{16,24},{1,9},{9,17},{17,25},{2,10},{10,18},{18,26},{... | collective-permute-start | bytes 24776 | tf_op jit(solution)/shard_map/ppermute | solution.py:16
  945.3 7.1 collective-permute-start.44
  945.8 8.3 collective-permute-start.45
  954.2 6.4 collective-permute-start.46
  964.1 8.7 collective-permute-start.49
  (128 other events, 5122.6 us)
where the time goes:
time: 984 us; the launch traced here: 976 us
  blocking collectives  685 us (70%)
  starting transfers between devices  94.2 us (10%)
  waiting for transfers between devices  89.3 us (9%)
  other arithmetic  58.4 us (6%)
  between operations  37.4 us (4%)
  local copies, waits for them, and re-layouts  11.3 us (1%)
    psum x6, blocking collectives, smoothed_terms(): lax.psum((jnp.sum(residual * precond), jnp.sum(precond * smooth)), ('lat'...  239 us
    psum x5, blocking collectives, body(): lax.psum(jnp.sum(res_new * image, axis=(1, 2)), ('lat', 'lon'))  209 us
    psum x5, blocking collectives, body(): lax.psum(jnp.sum(dir_bar * inner_dir, axis=(1, 2)), ('lat', 'lon'))  194 us
    ppermute x24, starting transfers between devices, padded_2(): lax.ppermute(lax.slice_in_dim(block, block.shape[dim] - width, None, axis...  63.2 us
    ppermute x24, waiting for transfers between devices, padded_2(): lax.ppermute(lax.slice_in_dim(block, 0, width, axis=dim), axis, backward)  45.4 us
    psum x1, blocking collectives, body(): lax.psum(jnp.stack([jnp.sum(cost_weights * padded_dirs[step][1:-1, 1:-1],...  42.9 us
    ppermute x24, waiting for transfers between devices, padded_2(): lax.ppermute(lax.slice_in_dim(block, block.shape[dim] - width, None, axis...  41.3 us
    ppermute x24, starting transfers between devices, padded_2(): lax.ppermute(lax.slice_in_dim(block, 0, width, axis=dim), axis, backward)  28.8 us
  transfers between devices with their start and end apart: 50, of which 32 were waited for; matrix products, arithmetic and copies ran while one was open for 0% of the time, Pallas kernels for 0%

commit v1 on v0

v1 whole, which is shorter than its diff:
```python
import functools

import jax
import jax.numpy as jnp
from jax import lax
from jax.experimental import pallas as pl
from jax.experimental.pallas import tpu as pltpu
from jax.sharding import PartitionSpec as P

ITERS = 6
MESH = pl.DeviceIdType.MESH
HR = 16
HB = 8
HC = 13
HW = 6


def cost_of(mu, proj):
    def dot(a, b):
        acc = [None] * (len(a) + len(b) - 1)
        for i, x in enumerate(a):
            for j, y in enumerate(b):
                if a is b and j < i:
                    continue
                pr = x * y
                if a is b and j > i:
                    pr = pr + pr
                for m in (i + j, abs(i - j)):
                    acc[m] = pr if acc[m] is None else acc[m] + pr
        tot = acc[0] * mu[0]
        for m in range(1, len(acc)):
            tot = tot + acc[m] * mu[m]
        return 0.5 * tot

    def apply(p):
        q = list(p) + [None]
        for k, x in enumerate(p):
            if k == 0:
                q[1] = -x if q[1] is None else q[1] - x
            else:
                hx = 0.5 * x
                q[k + 1] = -hx if q[k + 1] is None else q[k + 1] - hx
                q[k - 1] = q[k - 1] - hx
        return q

    one = jnp.ones_like(mu[0])
    z, p, rz, cost = [one], [one], mu[0], None
    for step in range(ITERS):
        q = apply(p)
        alpha = rz / dot(p, q)
        term = p[0] * proj[0]
        for k in range(1, len(p)):
            term = term + p[k] * proj[k]
        cost = alpha * term if cost is None else cost + alpha * term
        if step < ITERS - 1:
            z = [z[k] - alpha * q[k] for k in range(len(z))] + [-alpha * q[-1]]
            rz_new = dot(z, z)
            beta = rz_new / rz
            p = [z[k] + beta * p[k] for k in range(len(p))] + [z[-1]]
            rz = rz_new
    return cost


def roll(x, shift, axis):
    return pltpu.roll(x, shift % x.shape[axis], axis)


def east(x):
    return roll(x, -1, 1)


def north(x):
    return roll(x, -1, 0)


def kernel(nlat, nlon, names, f_ref, de_ref, dn_ref, st_ref, mk_ref, w_ref, fa_ref, ge_ref, gn_ref,
           send_w, send_e, recv_e, recv_w, row_n, row_s, mrow_n, mrow_s, wrow_n, wrow_s,
           part, part2, got_lon, got_lat, sums, wp, coef,
           ssem, rsem, ss_lon, rs_lon, ss_lat, rs_lat):
    lat, lon = lax.axis_index("lat"), lax.axis_index("lon")
    costs, rows, cols = w_ref.shape

    def peer(dlat, dlon):
        return (lax.rem(lat + dlat + nlat, nlat), lax.rem(lon + dlon + nlon, nlon))

    peers = {(a % nlat, b % nlon) for a in (-1, 0, 1) for b in (-1, 0, 1)}
    peers |= {(0, b) for b in range(nlon)} | {(a, 0) for a in range(nlat)}
    peers = sorted(peers - {(0, 0)})
    barrier = pltpu.get_barrier_semaphore()
    for a, b in peers:
        pl.semaphore_signal(barrier, inc=1, device_id=peer(a, b), device_id_type=MESH)

    lane = lax.broadcasted_iota(jnp.int32, (rows, 128), 1)
    wide = [f_ref, de_ref, dn_ref, st_ref, mk_ref]
    for ref, at, first in ((send_w, slice(0, 128), True), (send_e, slice(cols - 128, cols), False)):
        buf = jnp.zeros((rows, 128), jnp.float32)
        pos = 0
        for i in range(5 + costs):
            width = HC if i < 5 else HW
            tile = (wide[i][:, at] if i < 5 else w_ref[i - 5, :, at]).astype(jnp.float32)
            tile = roll(tile, pos if first else pos + width, 1)
            buf = jnp.where((lane >= pos) & (lane < pos + width), tile, buf)
            pos += width
        ref[...] = buf
    pl.semaphore_wait(barrier, len(peers))

    copies = []

    def send(src, dst, dev):
        i = len(copies)
        c = pltpu.make_async_remote_copy(src_ref=src, dst_ref=dst, send_sem=ssem.at[i],
                                         recv_sem=rsem.at[i], device_id=dev, device_id_type=MESH)
        c.start()
        copies.append(c)

    lo, hi = pl.ds(0, HR), pl.ds(rows - HR, HR)
    for src, dst, d in ((send_w, recv_e, -1), (send_e, recv_w, 1)):
        send(src.at[lo], dst.at[pl.ds(rows, HR)], peer(-1, d))
        send(src.at[hi], dst.at[pl.ds(rows + HR, HR)], peer(1, d))
        send(src, dst.at[pl.ds(0, rows)], peer(0, d))
    for i in range(5):
        src = wide[i]
        send(src.at[lo], row_n.at[i] if i < 4 else mrow_n, peer(-1, 0))
        send(src.at[hi], row_s.at[i] if i < 4 else mrow_s, peer(1, 0))
    early = len(copies)
    send(w_ref.at[:, pl.ds(0, HB)], wrow_n, peer(-1, 0))
    send(w_ref.at[:, pl.ds(rows - HB, HB)], wrow_s, peer(1, 0))
    for c in copies[:early]:
        c.wait_recv()

    full = rows + 2 * HR
    lane = lax.broadcasted_iota(jnp.int32, (full, 128), 1)
    got_e, got_w = recv_e[...], recv_w[...]

    def side(pos, width):
        a = roll(got_e, -pos, 1)
        b = roll(got_w, 128 - width - pos, 1)
        return jnp.where(lane < width, a, jnp.where(lane >= 128 - width, b, 0.0))

    def padded(i):
        if i < 4:
            top, mid, low = row_n[i], wide[i][...], row_s[i]
        else:
            top, mid, low = (r[...].astype(jnp.float32) for r in (mrow_n, mk_ref, mrow_s))
        return jnp.concatenate([jnp.concatenate([mid, top, low], axis=0), side(HC * i, HC)], axis=1)

    ringc = cols + 128
    row_id = lax.broadcasted_iota(jnp.int32, (full, ringc), 0)
    keep_n = (lat < nlat - 1).astype(jnp.float32)
    keep_s = (lat > 0).astype(jnp.float32)
    edge = jnp.where(row_id < rows, 1.0, jnp.where(row_id < rows + HR, keep_n, keep_s))
    wet = padded(4) * edge
    ex = padded(1) * wet * east(wet)
    ey = padded(2) * wet * north(wet)
    base = wet * padded(3) + 1.0 - wet
    diag = base + ex + roll(ex, 1, 1) + ey + roll(ey, 1, 0)
    rs = lax.rsqrt(diag)
    rs = rs * (1.5 - 0.5 * diag * rs * rs)
    rs_e, rs_n = rs * east(rs), rs * north(rs)
    e2 = 2.0 * ex * rs_e
    n2 = 2.0 * ey * rs_n

    def twice(v, e2, n2):
        return e2 * east(v) + roll(e2 * v, 1, 1) + n2 * north(v) + roll(n2 * v, 1, 0)

    us = [rs * padded(0)]
    us.append(0.5 * twice(us[0], e2, n2))
    for k in range(1, ITERS):
        us.append(twice(us[k], e2, n2) - us[k - 1])

    inner = [u[:rows, :cols] for u in us]
    rs_in = rs[:rows, :cols]

    def put(at, field):
        line = jnp.sum(field, axis=0, keepdims=True)
        tot = line[:, :128]
        for c in range(128, cols, 128):
            tot = tot + line[:, c:c + 128]
        sums[at:at + 1, :] = tot

    sums[...] = jnp.zeros_like(sums)
    mom = ITERS * costs
    for k in range(ITERS):
        put(mom + 2 * k, inner[k] * inner[k])
        put(mom + 2 * k + 1, inner[k] * inner[k + 1])
    for n in range(costs):
        wn = w_ref[n] * rs_in
        for k in range(ITERS):
            put(k * costs + n, wn * inner[k])
    nsum = sums.shape[0]
    lane_s = lax.broadcasted_iota(jnp.int32, (nsum, 128), 1)
    row_s_id = lax.broadcasted_iota(jnp.int32, (nsum, 128), 0)
    by_row = jnp.sum(sums[...], axis=1, keepdims=True)
    mine = jnp.sum(jnp.where(lane_s == row_s_id, by_row, 0.0), axis=0, keepdims=True)
    part[...] = mine
    lon_copies = []
    for d in range(1, nlon):
        c = pltpu.make_async_remote_copy(src_ref=part, dst_ref=got_lon.at[d - 1],
                                         send_sem=ss_lon.at[d - 1], recv_sem=rs_lon.at[d - 1],
                                         device_id=peer(0, d), device_id_type=MESH)
        c.start()
        lon_copies.append(c)

    for c in copies[early:]:
        c.wait_recv()

    def cut(x):
        return jnp.concatenate([x[:rows + HB], x[full - HB:]], axis=0)

    rs_b = cut(rs)
    for n in range(costs):
        block = jnp.concatenate([w_ref[n], wrow_n[n], wrow_s[n]], axis=0)
        tile = cut(side(5 * HC + HW * n, HW))
        wp[n] = rs_b * jnp.concatenate([block, tile], axis=1)
    e2b, n2b = cut(e2), cut(n2)
    ub = [cut(u) for u in us]

    for c in lon_copies:
        c.wait_recv()
    total = mine
    for d in range(1, nlon):
        total = total + got_lon[d - 1]
    part2[...] = total
    lat_copies = []
    for d in range(1, nlat):
        c = pltpu.make_async_remote_copy(src_ref=part2, dst_ref=got_lat.at[d - 1],
                                         send_sem=ss_lat.at[d - 1], recv_sem=rs_lat.at[d - 1],
                                         device_id=peer(d, 0), device_id_type=MESH)
        c.start()
        lat_copies.append(c)
    for c in lat_copies:
        c.wait_recv()
    for d in range(1, nlat):
        total = total + got_lat[d - 1]

    tot8 = jnp.broadcast_to(total, (costs, 128))
    lane8 = lax.broadcasted_iota(jnp.int32, (costs, 128), 1)
    sub8 = lax.broadcasted_iota(jnp.int32, (costs, 128), 0)

    def pick(index):
        return jnp.broadcast_to(
            jnp.sum(jnp.where(lane8 == index, tot8, 0.0), axis=1, keepdims=True), (costs, 128))

    proj = [pick(k * costs + sub8) for k in range(ITERS)]
    raw = [pick(mom + m) for m in range(2 * ITERS)]
    mu = [raw[0], raw[1]]
    for k in range(1, ITERS):
        mu += [2.0 * raw[2 * k] - raw[0], 2.0 * raw[2 * k + 1] - raw[1]]
    cost, pull = jax.vjp(cost_of, mu, proj)
    mu_bar, x = pull(jnp.ones_like(cost))
    even = [2.0 * mu_bar[2 * k] for k in range(ITERS)]
    odd = [2.0 * mu_bar[2 * k + 1] for k in range(ITERS)]
    even[0] = mu_bar[0] - 0.5 * sum(even[1:])
    odd[0] = mu_bar[1] - 0.5 * sum(odd[1:])
    reps = ringc // 128
    for k in range(ITERS):
        for i, v in enumerate((x[k], 2.0 * even[k], odd[k])):
            coef[3 * k + i] = jnp.concatenate([v] * reps, axis=1)

    u_half = [0.5 * u for u in ub]
    ug = [u_half[0]] + ub[1:]
    u_in = [u[:rows, :cols] for u in ug]
    u_east = [east(u)[:rows, :cols] for u in ug]
    u_north = [north(u)[:rows, :cols] for u in ug]
    quad = [ub[0], ub[1]] + [ub[k] + ub[k - 2] for k in range(2, ITERS)] + [u_half[6] + ub[4]]
    wet_in = wet[:rows, :cols]
    me = wet_in * east(wet)[:rows, :cols]
    mn = wet_in * north(wet)[:rows, :cols]
    mre = 2.0 * me * rs_e[:rows, :cols]
    mrn = 2.0 * mn * rs_n[:rows, :cols]
    neg = -(rs_b * rs_b)

    def one(n, carry):
        def c(i):
            return coef[i, pl.ds(n, 1), :]

        wn = wp[n]
        nxt = c(3 * 5 + 2) * ub[5]
        nxt2 = None
        dd = nxt * quad[6]
        eb = nb = None
        for k in range(ITERS - 1, -1, -1):
            le, ln = east(nxt), north(nxt)
            s2 = e2b * le + roll(e2b * nxt, 1, 1) + n2b * ln + roll(n2b * nxt, 1, 0)
            if k == 0:
                s2 = 0.5 * s2
            lin = nxt[:rows, :cols]
            ea = lin * u_east[k] + le[:rows, :cols] * u_in[k]
            na = lin * u_north[k] + ln[:rows, :cols] * u_in[k]
            eb = ea if eb is None else eb + ea
            nb = na if nb is None else nb + na
            seed = c(3 * k + 1) * ub[k] + c(3 * k + 2) * ub[k + 1]
            if k > 0:
                seed = seed + c(3 * k - 1) * ub[k - 1]
            lam = c(3 * k) * wn + seed + s2
            if nxt2 is not None:
                lam = lam - nxt2
            dd = dd + lam * quad[k] - seed * u_half[k]
            nxt, nxt2 = lam, nxt
        fa_ref[n] = rs_in * nxt[:rows, :cols]
        db = neg * dd
        db_in = db[:rows, :cols]
        ge_ref[n] = mre * eb + me * (db_in + east(db)[:rows, :cols])
        gn_ref[n] = mrn * nb + mn * (db_in + north(db)[:rows, :cols])
        return carry

    lax.fori_loop(0, costs, one, 0)
    for c in copies + lon_copies + lat_copies:
        c.wait_send()


def solution(mesh):
    nlat, nlon = mesh.shape["lat"], mesh.shape["lon"]

    def body(forcing, depth_east, depth_north, surface_term, ocean_mask, cost_weights):
        costs, rows, cols = cost_weights.shape
        full, ringc = rows + 2 * HR, cols + 128
        f32 = jnp.float32
        dma = pltpu.SemaphoreType.DMA
        nsum = -(-(ITERS * costs + 2 * ITERS) // 8) * 8
        vmem = pl.BlockSpec(memory_space=pltpu.VMEM)
        return pl.pallas_call(
            functools.partial(kernel, nlat, nlon, None),
            out_shape=[jax.ShapeDtypeStruct((costs, rows, cols), f32)] * 3,
            in_specs=[vmem] * 6,
            out_specs=[vmem] * 3,
            scratch_shapes=[
                pltpu.VMEM((rows, 128), f32),
                pltpu.VMEM((rows, 128), f32),
                pltpu.VMEM((full, 128), f32),
                pltpu.VMEM((full, 128), f32),
                pltpu.VMEM((4, HR, cols), f32),
                pltpu.VMEM((4, HR, cols), f32),
                pltpu.VMEM((HR, cols), jnp.int32),
                pltpu.VMEM((HR, cols), jnp.int32),
                pltpu.VMEM((costs, HB, cols), f32),
                pltpu.VMEM((costs, HB, cols), f32),
                pltpu.VMEM((1, 128), f32),
                pltpu.VMEM((1, 128), f32),
                pltpu.VMEM((nlon - 1, 1, 128), f32),
                pltpu.VMEM((nlat - 1, 1, 128), f32),
                pltpu.VMEM((nsum, 128), f32),
                pltpu.VMEM((costs, rows + 2 * HB, ringc), f32),
                pltpu.VMEM((3 * ITERS, costs, ringc), f32),
                dma((18,)),
                dma((18,)),
                dma((nlon - 1,)),
                dma((nlon - 1,)),
                dma((nlat - 1,)),
                dma((nlat - 1,)),
            ],
            compiler_params=pltpu.CompilerParams(
                collective_id=0, has_side_effects=True, vmem_limit_bytes=48 * 1024 * 1024
            ),
        )(forcing, depth_east, depth_north, surface_term, ocean_mask, cost_weights)

    grid = P("lat", "lon")
    field = P(None, "lat", "lon")
    return jax.shard_map(
        body,
        mesh=mesh,
        in_specs=(grid, grid, grid, grid, grid, field),
        out_specs=(field, field, field),
        check_vma=False,
    )
```

time: 984 us -> 38.7 us (0.04)
  blocking collectives: 685 us -> 0 us
  starting transfers between devices: 94.2 us -> 0 us
  waiting for transfers between devices: 89.3 us -> 0 us
  other arithmetic: 58.4 us -> 0 us
  between operations: 37.4 us -> 0.65 us
  Pallas kernels: 0 us -> 30.1 us
    psum x17 -> x0, blocking collectives: 685 us -> none  [the longest x6 239 us: smoothed_terms(): lax.psum((jnp.sum(residual * precond), jnp.sum(precond * smooth)), ('lat'...]
    ppermute x50 -> x0, starting transfers between devices: 94.2 us -> none  [the longest x24 63.2 us: padded_2(): lax.ppermute(lax.slice_in_dim(block, block.shape[dim] - width, None, axis...]
    ppermute x50 -> x0, waiting for transfers between devices: 89.3 us -> none  [the longest x24 45.4 us: padded_2(): lax.ppermute(lax.slice_in_dim(block, 0, width, axis=dim), axis, backward)]
    pallas_call x0 -> x1, Pallas kernels: none -> 30.1 us  [body(): pl.pallas_call(functools.partial(kernel, nlat, nlon, None), out_shape=[ja...]
    reduce_sum x17 -> x0, other arithmetic: 25.3 us -> none  [the longest x5 12.5 us: body(): jnp.sum(dir_bar * inner_dir, axis=(1, 2))]
    mul x13 -> x0, other arithmetic: 19.2 us -> none  [the longest x5 11 us: body(): 2.0 * norm_next_bar[:, None, None] * precond_next]
  transfers between devices with their start and end apart: 50 -> 0, of which waited for: 32 -> 0; matrix products, arithmetic and copies ran while one was open for 0% -> 0% of each run, Pallas kernels for 0% -> 0%
where the time goes in v1:
time: 38.7 us; the launch traced here: 38.3 us
  Pallas kernels  30.1 us (78%)
  local copies, waits for them, and re-layouts  7.61 us (20%)
  between operations  0.65 us (2%)
    pallas_call x1, Pallas kernels, body(): pl.pallas_call(functools.partial(kernel, nlat, nlon, None), out_shape=[ja...  30.1 us
    unnamed x15, local copies, waits for them, and re-layouts  7.61 us

profile of v1, /device:TPU:0, one launch (start us, length us, event | category | flops | bytes accessed | tf_op | source)
XLA Modules:
  0.0 38.3 jit_solution(1126073730941455415)
XLA Ops:
  0.6 0.0 copy-start
  0.6 1.0 %copy-done = f32[8,64,256]{2,1,0:T(8,128)S(1)} copy-done((f32[8,64,256]{2,1,0:T(8,128)S(1)}, f32[8,64,256]{2,1,0:T(8,128)}, u32[]{:S(2)}) %copy-start) | copy-done | bytes 524312
  1.7 0.0 copy-start.1
  1.7 0.8 %copy-done.1 = f32[64,256]{1,0:T(8,128)S(1)} copy-done((f32[64,256]{1,0:T(8,128)S(1)}, f32[64,256]{1,0:T(8,128)}, u32[]{:S(2)}) %copy-start.1) | copy-done | bytes 65560
  2.5 0.0 copy-start.2
  2.5 0.8 %copy-done.2 = f32[64,256]{1,0:T(8,128)S(1)} copy-done((f32[64,256]{1,0:T(8,128)S(1)}, f32[64,256]{1,0:T(8,128)}, u32[]{:S(2)}) %copy-start.2) | copy-done | bytes 65560
  3.4 0.0 copy-start.3
  3.4 0.8 %copy-done.3 = f32[64,256]{1,0:T(8,128)S(1)} copy-done((f32[64,256]{1,0:T(8,128)S(1)}, f32[64,256]{1,0:T(8,128)}, u32[]{:S(2)}) %copy-start.3) | copy-done | bytes 65560
  4.2 0.0 copy-start.4
  4.2 0.8 %copy-done.4 = f32[64,256]{1,0:T(8,128)S(1)} copy-done((f32[64,256]{1,0:T(8,128)S(1)}, f32[64,256]{1,0:T(8,128)}, u32[]{:S(2)}) %copy-start.4) | copy-done | bytes 65560
  5.0 0.0 copy-start.5
  5.0 0.8 %copy-done.5 = s32[64,256]{1,0:T(8,128)S(1)} copy-done((s32[64,256]{1,0:T(8,128)S(1)}, s32[64,256]{1,0:T(8,128)}, u32[]{:S(2)}) %copy-start.5) | copy-done | bytes 65560
  5.9 30.1 %shard_map.85 = (f32[8,64,256]{2,1,0:T(8,128)S(1)}, f32[8,64,256]{2,1,0:T(8,128)S(1)}, f32[8,64,256]{2,1,0:T(8,128)S(1)}) custom-call(f32[64,256]{1,0:T(8,128)S(1)} %copy-done.1, f32[64,256]{1,0:T(8,128)S(1)} %copy-done.2, f32[64,256]{1,0:T(8,128)S(1)} %copy-done.3, f32[64,256]{1,0:T(8,128)S(1)} %copy-done.4, s32[64,256]{1,0:T(8,128)S(1)} %copy-done.5, ...), custom_call_target="tpu_custom_call" | custom-call | tf_op jit(solution)/shard_map/pallas_call | solution.py:322
  36.0 0.8 %copy.12 = f32[8,64,256]{2,1,0:T(8,128)} copy(f32[8,64,256]{2,1,0:T(8,128)S(1)} %get-tuple-element.6) | data formatting | bytes 1048576
  36.8 0.8 %copy.13 = f32[8,64,256]{2,1,0:T(8,128)} copy(f32[8,64,256]{2,1,0:T(8,128)S(1)} %get-tuple-element.7) | data formatting | bytes 1048576
  37.5 0.8 %copy.14 = f32[8,64,256]{2,1,0:T(8,128)} copy(f32[8,64,256]{2,1,0:T(8,128)S(1)} %get-tuple-element.8) | data formatting | bytes 1048576
Async XLA Ops:
  0.6 1.0 %copy-start = (f32[8,64,256]{2,1,0:T(8,128)S(1)}, f32[8,64,256]{2,1,0:T(8,128)}, u32[]{:S(2)}) copy-start(f32[8,64,256]{2,1,0:T(8,128)} %w_ref.1) | copy-start | bytes 1572868
  1.7 0.8 %copy-start.1 = (f32[64,256]{1,0:T(8,128)S(1)}, f32[64,256]{1,0:T(8,128)}, u32[]{:S(2)}) copy-start(f32[64,256]{1,0:T(8,128)} %f_ref.1) | copy-start | bytes 196612
  2.5 0.8 %copy-start.2 = (f32[64,256]{1,0:T(8,128)S(1)}, f32[64,256]{1,0:T(8,128)}, u32[]{:S(2)}) copy-start(f32[64,256]{1,0:T(8,128)} %de_ref.1) | copy-start | bytes 196612
  3.4 0.8 %copy-start.3 = (f32[64,256]{1,0:T(8,128)S(1)}, f32[64,256]{1,0:T(8,128)}, u32[]{:S(2)}) copy-start(f32[64,256]{1,0:T(8,128)} %dn_ref.1) | copy-start | bytes 196612
  4.2 0.8 %copy-start.4 = (f32[64,256]{1,0:T(8,128)S(1)}, f32[64,256]{1,0:T(8,128)}, u32[]{:S(2)}) copy-start(f32[64,256]{1,0:T(8,128)} %st_ref.1) | copy-start | bytes 196612
  5.0 0.8 %copy-start.5 = (s32[64,256]{1,0:T(8,128)S(1)}, s32[64,256]{1,0:T(8,128)}, u32[]{:S(2)}) copy-start(s32[64,256]{1,0:T(8,128)} %mk_ref.1) | copy-start | bytes 196612

commit v2 on v1

--- a/solution.py
+++ b/solution.py
@@ -73,22 +73,30 @@
     return roll(x, -1, 0)
 
 
-def kernel(nlat, nlon, names, f_ref, de_ref, dn_ref, st_ref, mk_ref, w_ref, fa_ref, ge_ref, gn_ref,
+def kernel(nlat, nlon, stages, f_hbm, de_hbm, dn_hbm, st_hbm, mk_hbm, w_hbm, fa_ref, ge_ref, gn_ref,
+           f_ref, de_ref, dn_ref, st_ref, mk_ref, w_ref, lsem,
            send_w, send_e, recv_e, recv_w, row_n, row_s, mrow_n, mrow_s, wrow_n, wrow_s,
-           part, part2, got_lon, got_lat, sums, wp, coef,
-           ssem, rsem, ss_lon, rs_lon, ss_lat, rs_lat):
+           sums, wp, coef, ssem, rsem, *reduce_refs):
     lat, lon = lax.axis_index("lat"), lax.axis_index("lon")
     costs, rows, cols = w_ref.shape
+    loads = [pltpu.make_async_copy(src, dst, lsem.at[i]) for i, (src, dst) in enumerate(
+        zip((f_hbm, de_hbm, dn_hbm, st_hbm, mk_hbm, w_hbm),
+            (f_ref, de_ref, dn_ref, st_ref, mk_ref, w_ref)))]
+    for c in loads:
+        c.start()
 
     def peer(dlat, dlon):
         return (lax.rem(lat + dlat + nlat, nlat), lax.rem(lon + dlon + nlon, nlon))
 
     peers = {(a % nlat, b % nlon) for a in (-1, 0, 1) for b in (-1, 0, 1)}
-    peers |= {(0, b) for b in range(nlon)} | {(a, 0) for a in range(nlat)}
+    peers |= {o for stage in stages for o in stage}
     peers = sorted(peers - {(0, 0)})
     barrier = pltpu.get_barrier_semaphore()
     for a, b in peers:
         pl.semaphore_signal(barrier, inc=1, device_id=peer(a, b), device_id_type=MESH)
+
+    for c in loads:
+        c.wait()
 
     lane = lax.broadcasted_iota(jnp.int32, (rows, 128), 1)
     wide = [f_ref, de_ref, dn_ref, st_ref, mk_ref]
@@ -192,14 +200,29 @@
     row_s_id = lax.broadcasted_iota(jnp.int32, (nsum, 128), 0)
     by_row = jnp.sum(sums[...], axis=1, keepdims=True)
     mine = jnp.sum(jnp.where(lane_s == row_s_id, by_row, 0.0), axis=0, keepdims=True)
-    part[...] = mine
-    lon_copies = []
-    for d in range(1, nlon):
-        c = pltpu.make_async_remote_copy(src_ref=part, dst_ref=got_lon.at[d - 1],
-                                         send_sem=ss_lon.at[d - 1], recv_sem=rs_lon.at[d - 1],
-                                         device_id=peer(0, d), device_id_type=MESH)
-        c.start()
-        lon_copies.append(c)
+    reduce_copies = []
+
+    def start(stage, value):
+        mailbox, got, ss, rv = reduce_refs[4 * stage:4 * stage + 4]
+        mailbox[...] = value
+        group = []
+        for i, (a, b) in enumerate(stages[stage]):
+            c = pltpu.make_async_remote_copy(src_ref=mailbox, dst_ref=got.at[i], send_sem=ss.at[i],
+                                             recv_sem=rv.at[i], device_id=peer(a, b),
+                                             device_id_type=MESH)
+            c.start()
+            group.append(c)
+        reduce_copies.extend(group)
+        return group
+
+    def finish(stage, group, value):
+        for c in group:
+            c.wait_recv()
+        for i in range(len(group)):
+            value = value + reduce_refs[4 * stage + 1][i]
+        return value
+
+    group = start(0, mine)
 
     for c in copies[early:]:
         c.wait_recv()
@@ -215,23 +238,21 @@
     e2b, n2b = cut(e2), cut(n2)
     ub = [cut(u) for u in us]
 
-    for c in lon_copies:
-        c.wait_recv()
-    total = mine
-    for d in range(1, nlon):
-        total = total + got_lon[d - 1]
-    part2[...] = total
-    lat_copies = []
-    for d in range(1, nlat):
-        c = pltpu.make_async_remote_copy(src_ref=part2, dst_ref=got_lat.at[d - 1],
-                                         send_sem=ss_lat.at[d - 1], recv_sem=rs_lat.at[d - 1],
-                                         device_id=peer(d, 0), device_id_type=MESH)
-        c.start()
-        lat_copies.append(c)
-    for c in lat_copies:
-        c.wait_recv()
-    for d in range(1, nlat):
-        total = total + got_lat[d - 1]
+    ug = [0.5 * ub[0]] + ub[1:]
+    u_in = [u[:rows, :cols] for u in ug]
+    u_east = [east(u)[:rows, :cols] for u in ug]
+    u_north = [north(u)[:rows, :cols] for u in ug]
+    quad = [ub[0], ub[1]] + [ub[k] + ub[k - 2] for k in range(2, ITERS)] + [0.5 * ub[6] + ub[4]]
+    wet_in = wet[:rows, :cols]
+    me = wet_in * east(wet)[:rows, :cols]
+    mn = wet_in * north(wet)[:rows, :cols]
+    mre = 2.0 * me * rs_e[:rows, :cols]
+    mrn = 2.0 * mn * rs_n[:rows, :cols]
+    neg = -(rs_b * rs_b)
+
+    total = finish(0, group, mine)
+    for stage in range(1, len(stages)):
+        total = finish(stage, start(stage, total), total)
 
     tot8 = jnp.broadcast_to(total, (costs, 128))
     lane8 = lax.broadcasted_iota(jnp.int32, (costs, 128), 1)
@@ -257,19 +278,6 @@
         for i, v in enumerate((x[k], 2.0 * even[k], odd[k])):
             coef[3 * k + i] = jnp.concatenate([v] * reps, axis=1)
 
-    u_half = [0.5 * u for u in ub]
-    ug = [u_half[0]] + ub[1:]
-    u_in = [u[:rows, :cols] for u in ug]
-    u_east = [east(u)[:rows, :cols] for u in ug]
-    u_north = [north(u)[:rows, :cols] for u in ug]
-    quad = [ub[0], ub[1]] + [ub[k] + ub[k - 2] for k in range(2, ITERS)] + [u_half[6] + ub[4]]
-    wet_in = wet[:rows, :cols]
-    me = wet_in * east(wet)[:rows, :cols]
-    mn = wet_in * north(wet)[:rows, :cols]
-    mre = 2.0 * me * rs_e[:rows, :cols]
-    mrn = 2.0 * mn * rs_n[:rows, :cols]
-    neg = -(rs_b * rs_b)
-
     def one(n, carry):
         def c(i):
             return coef[i, pl.ds(n, 1), :]
@@ -278,7 +286,7 @@
         nxt = c(3 * 5 + 2) * ub[5]
         nxt2 = None
         dd = nxt * quad[6]
-        eb = nb = None
+        eb = nb = du = None
         for k in range(ITERS - 1, -1, -1):
             le, ln = east(nxt), north(nxt)
             s2 = e2b * le + roll(e2b * nxt, 1, 1) + n2b * ln + roll(n2b * nxt, 1, 0)
@@ -295,17 +303,18 @@
             lam = c(3 * k) * wn + seed + s2
             if nxt2 is not None:
                 lam = lam - nxt2
-            dd = dd + lam * quad[k] - seed * u_half[k]
+            dd = dd + lam * quad[k]
+            du = seed * ub[k] if du is None else du + seed * ub[k]
             nxt, nxt2 = lam, nxt
         fa_ref[n] = rs_in * nxt[:rows, :cols]
-        db = neg * dd
+        db = neg * (dd - 0.5 * du)
         db_in = db[:rows, :cols]
         ge_ref[n] = mre * eb + me * (db_in + east(db)[:rows, :cols])
         gn_ref[n] = mrn * nb + mn * (db_in + north(db)[:rows, :cols])
         return carry
 
     lax.fori_loop(0, costs, one, 0)
-    for c in copies + lon_copies + lat_copies:
+    for c in copies + reduce_copies:
         c.wait_send()
 
 
@@ -318,13 +327,24 @@
         f32 = jnp.float32
         dma = pltpu.SemaphoreType.DMA
         nsum = -(-(ITERS * costs + 2 * ITERS) // 8) * 8
+        every = [(a, b) for a in range(nlat) for b in range(nlon) if a or b]
+        stages = [every] if len(every) < 64 else [
+            [(0, b) for b in range(1, nlon)], [(a, 0) for a in range(1, nlat)]]
+        reduce_scratch = [
+            ref for g in stages for ref in (
+                pltpu.VMEM((1, 128), f32), pltpu.VMEM((len(g), 1, 128), f32),
+                dma((len(g),)), dma((len(g),)))]
         vmem = pl.BlockSpec(memory_space=pltpu.VMEM)
         return pl.pallas_call(
-            functools.partial(kernel, nlat, nlon, None),
+            functools.partial(kernel, nlat, nlon, stages),
             out_shape=[jax.ShapeDtypeStruct((costs, rows, cols), f32)] * 3,
-            in_specs=[vmem] * 6,
+            in_specs=[pl.BlockSpec(memory_space=pltpu.HBM)] * 6,
             out_specs=[vmem] * 3,
             scratch_shapes=[
+                *[pltpu.VMEM((rows, cols), f32)] * 4,
+                pltpu.VMEM((rows, cols), jnp.int32),
+                pltpu.VMEM((costs, rows, cols), f32),
+                dma((6,)),
                 pltpu.VMEM((rows, 128), f32),
                 pltpu.VMEM((rows, 128), f32),
                 pltpu.VMEM((full, 128), f32),
@@ -335,22 +355,15 @@
                 pltpu.VMEM((HR, cols), jnp.int32),
                 pltpu.VMEM((costs, HB, cols), f32),
                 pltpu.VMEM((costs, HB, cols), f32),
-                pltpu.VMEM((1, 128), f32),
-                pltpu.VMEM((1, 128), f32),
-                pltpu.VMEM((nlon - 1, 1, 128), f32),
-                pltpu.VMEM((nlat - 1, 1, 128), f32),
                 pltpu.VMEM((nsum, 128), f32),
                 pltpu.VMEM((costs, rows + 2 * HB, ringc), f32),
                 pltpu.VMEM((3 * ITERS, costs, ringc), f32),
                 dma((18,)),
                 dma((18,)),
-                dma((nlon - 1,)),
-                dma((nlon - 1,)),
-                dma((nlat - 1,)),
-                dma((nlat - 1,)),
+                *reduce_scratch,
             ],
             compiler_params=pltpu.CompilerParams(
-                collective_id=0, has_side_effects=True, vmem_limit_bytes=48 * 1024 * 1024
+                collective_id=0, has_side_effects=True, vmem_limit_bytes=63 * 1024 * 1024
             ),
         )(forcing, depth_east, depth_north, surface_term, ocean_mask, cost_weights)
 

time: 38.7 us -> 34.5 us (0.89)
  local copies, waits for them, and re-layouts: 7.61 us -> 3.95 us
  Pallas kernels: 30.1 us -> 29.6 us
    unnamed x15 -> x7, local copies, waits for them, and re-layouts: 7.61 us -> 3.95 us
    pallas_call x1, Pallas kernels: 30.1 us -> 29.6 us  [body(): pl.pallas_call(functools.partial(kernel, nlat, nlon, stages), out_shape=[...]
where the time goes in v2:
time: 34.5 us; the launch traced here: 34.3 us
  Pallas kernels  29.6 us (86%)
  local copies, waits for them, and re-layouts  3.95 us (11%)
  between operations  0.65 us (2%)
    pallas_call x1, Pallas kernels, body(): pl.pallas_call(functools.partial(kernel, nlat, nlon, stages), out_shape=[...  29.6 us
    unnamed x7, local copies, waits for them, and re-layouts  3.95 us

profile of v2, /device:TPU:0, one launch (start us, length us, event | category | flops | bytes accessed | tf_op | source)
XLA Modules:
  0.0 34.3 jit_solution(1185290691165706317)
XLA Ops:
  0.6 29.6 %shard_map.85 = (f32[8,64,256]{2,1,0:T(8,128)}, f32[8,64,256]{2,1,0:T(8,128)}, f32[8,64,256]{2,1,0:T(8,128)}) custom-call(f32[64,256]{1,0:T(8,128)} %f_hbm.1, f32[64,256]{1,0:T(8,128)} %de_hbm.1, f32[64,256]{1,0:T(8,128)} %dn_hbm.1, f32[64,256]{1,0:T(8,128)} %st_hbm.1, s32[64,256]{1,0:T(8,128)} %mk_hbm.1, f32[8,64,256]{2,1,0:T(8,128)} %w_hbm.1), custom_call_target="tpu_custom_call" | custom-call | tf_op jit(solution)/shard_map/pallas_call | solution.py:338
  30.3 0.0 copy-start.1
  30.3 1.9 %copy.12 = f32[8,64,256]{2,1,0:T(8,128)} copy(f32[8,64,256]{2,1,0:T(8,128)} %get-tuple-element.6) | data formatting | bytes 1048576
  32.2 0.0 copy-done.1
  32.2 0.0 copy-start
  32.2 0.8 %copy.13 = f32[8,64,256]{2,1,0:T(8,128)} copy(f32[8,64,256]{2,1,0:T(8,128)S(1)} %copy-done.1) | data formatting | bytes 1048576
  33.0 0.4 %copy-done = f32[8,64,256]{2,1,0:T(8,128)S(1)} copy-done((f32[8,64,256]{2,1,0:T(8,128)S(1)}, f32[8,64,256]{2,1,0:T(8,128)}, u32[]{:S(2)}) %copy-start) | copy-done | bytes 524312
  33.5 0.8 %copy.14 = f32[8,64,256]{2,1,0:T(8,128)} copy(f32[8,64,256]{2,1,0:T(8,128)S(1)} %copy-done) | data formatting | bytes 1048576
Async XLA Ops:
  30.3 1.9 %copy-start.1 = (f32[8,64,256]{2,1,0:T(8,128)S(1)}, f32[8,64,256]{2,1,0:T(8,128)}, u32[]{:S(2)}) copy-start(f32[8,64,256]{2,1,0:T(8,128)} %get-tuple-element.7) | copy-start | bytes 1572868
  32.2 1.2 %copy-start = (f32[8,64,256]{2,1,0:T(8,128)S(1)}, f32[8,64,256]{2,1,0:T(8,128)}, u32[]{:S(2)}) copy-start(f32[8,64,256]{2,1,0:T(8,128)} %get-tuple-element.8) | copy-start | bytes 1572868

commit v3 on v2

--- a/solution.py
+++ b/solution.py
@@ -73,10 +73,10 @@
     return roll(x, -1, 0)
 
 
-def kernel(nlat, nlon, stages, f_hbm, de_hbm, dn_hbm, st_hbm, mk_hbm, w_hbm, fa_ref, ge_ref, gn_ref,
+def kernel(nlat, nlon, stages, f_hbm, de_hbm, dn_hbm, st_hbm, mk_hbm, w_hbm, wp_out, pack_out, geo_out, coef_out,
            f_ref, de_ref, dn_ref, st_ref, mk_ref, w_ref, lsem,
            send_w, send_e, recv_e, recv_w, row_n, row_s, mrow_n, mrow_s, wrow_n, wrow_s,
-           sums, wp, coef, ssem, rsem, *reduce_refs):
+           sums, wp, pack, geo, coef, osem, ssem, rsem, *reduce_refs):
     lat, lon = lax.axis_index("lat"), lax.axis_index("lon")
     costs, rows, cols = w_ref.shape
     loads = [pltpu.make_async_copy(src, dst, lsem.at[i]) for i, (src, dst) in enumerate(
@@ -235,20 +235,19 @@
         block = jnp.concatenate([w_ref[n], wrow_n[n], wrow_s[n]], axis=0)
         tile = cut(side(5 * HC + HW * n, HW))
         wp[n] = rs_b * jnp.concatenate([block, tile], axis=1)
-    e2b, n2b = cut(e2), cut(n2)
-    ub = [cut(u) for u in us]
-
-    ug = [0.5 * ub[0]] + ub[1:]
-    u_in = [u[:rows, :cols] for u in ug]
-    u_east = [east(u)[:rows, :cols] for u in ug]
-    u_north = [north(u)[:rows, :cols] for u in ug]
-    quad = [ub[0], ub[1]] + [ub[k] + ub[k - 2] for k in range(2, ITERS)] + [0.5 * ub[6] + ub[4]]
+    for k in range(ITERS + 1):
+        pack[k] = cut(us[k])
+    pack[ITERS + 1], pack[ITERS + 2], pack[ITERS + 3] = cut(e2), cut(n2), rs_b
     wet_in = wet[:rows, :cols]
     me = wet_in * east(wet)[:rows, :cols]
     mn = wet_in * north(wet)[:rows, :cols]
-    mre = 2.0 * me * rs_e[:rows, :cols]
-    mrn = 2.0 * mn * rs_n[:rows, :cols]
-    neg = -(rs_b * rs_b)
+    geo[0], geo[1] = me, mn
+    geo[2] = 2.0 * me * rs_e[:rows, :cols]
+    geo[3] = 2.0 * mn * rs_n[:rows, :cols]
+    saves = [pltpu.make_async_copy(src, dst, osem.at[i]) for i, (src, dst) in enumerate(
+        ((pack, pack_out), (geo, geo_out), (wp, wp_out), (coef, coef_out)))]
+    for c in saves[:3]:
+        c.start()
 
     total = finish(0, group, mine)
     for stage in range(1, len(stages)):
@@ -273,19 +272,55 @@
     odd = [2.0 * mu_bar[2 * k + 1] for k in range(ITERS)]
     even[0] = mu_bar[0] - 0.5 * sum(even[1:])
     odd[0] = mu_bar[1] - 0.5 * sum(odd[1:])
-    reps = ringc // 128
     for k in range(ITERS):
-        for i, v in enumerate((x[k], 2.0 * even[k], odd[k])):
-            coef[3 * k + i] = jnp.concatenate([v] * reps, axis=1)
+        coef[3 * k], coef[3 * k + 1], coef[3 * k + 2] = x[k], 2.0 * even[k], odd[k]
+    saves[3].start()
+    for c in copies + reduce_copies:
+        c.wait_send()
+    for c in saves:
+        c.wait()
+
+
+def adjoint_kernel(wp_hbm, pack_hbm, geo_hbm, coef_hbm, fa_hbm, ge_hbm, gn_hbm,
+                   wp, pack, geo, coef, u_in, u_east, u_north, quad, fa_ref, ge_ref, gn_ref,
+                   lsem, wsem, osem):
+    costs, rows, cols = fa_ref.shape
+    ringc = wp.shape[2]
+    loads = [pltpu.make_async_copy(src, dst, lsem.at[i]) for i, (src, dst) in enumerate(
+        ((pack_hbm, pack), (coef_hbm, coef), (geo_hbm, geo)))]
+    for c in loads:
+        c.start()
+
+    def weight(n):
+        return pltpu.make_async_copy(wp_hbm.at[n], wp.at[n], wsem.at[n])
+
+    def results(n):
+        return [pltpu.make_async_copy(src.at[n], dst.at[n], osem.at[i, n])
+                for i, (src, dst) in enumerate(((fa_ref, fa_hbm), (ge_ref, ge_hbm), (gn_ref, gn_hbm)))]
+
+    for n in range(costs):
+        weight(n).start()
+    for c in loads:
+        c.wait()
+    for k in range(ITERS):
+        u = pack[k] if k else 0.5 * pack[0]
+        u_in[k] = u[:rows, :cols]
+        u_east[k] = east(u)[:rows, :cols]
+        u_north[k] = north(u)[:rows, :cols]
+        quad[k] = pack[k] + pack[k - 2] if k > 1 else pack[k]
+    quad[ITERS] = 0.5 * pack[ITERS] + pack[ITERS - 2]
 
     def one(n, carry):
         def c(i):
-            return coef[i, pl.ds(n, 1), :]
-
+            return jnp.concatenate([coef[i, pl.ds(n, 1), :]] * (ringc // 128), axis=1)
+
+        weight(n).wait()
         wn = wp[n]
-        nxt = c(3 * 5 + 2) * ub[5]
+        ub = [pack.at[k] for k in range(ITERS + 1)]
+        e2b, n2b = pack[ITERS + 1], pack[ITERS + 2]
+        nxt = c(3 * ITERS - 1) * ub[ITERS - 1][...]
         nxt2 = None
-        dd = nxt * quad[6]
+        dd = nxt * quad[ITERS]
         eb = nb = du = None
         for k in range(ITERS - 1, -1, -1):
             le, ln = east(nxt), north(nxt)
@@ -297,25 +332,29 @@
             na = lin * u_north[k] + ln[:rows, :cols] * u_in[k]
             eb = ea if eb is None else eb + ea
             nb = na if nb is None else nb + na
-            seed = c(3 * k + 1) * ub[k] + c(3 * k + 2) * ub[k + 1]
+            seed = c(3 * k + 1) * ub[k][...] + c(3 * k + 2) * ub[k + 1][...]
             if k > 0:
-                seed = seed + c(3 * k - 1) * ub[k - 1]
+                seed = seed + c(3 * k - 1) * ub[k - 1][...]
             lam = c(3 * k) * wn + seed + s2
             if nxt2 is not None:
                 lam = lam - nxt2
             dd = dd + lam * quad[k]
-            du = seed * ub[k] if du is None else du + seed * ub[k]
+            du = seed * ub[k][...] if du is None else du + seed * ub[k][...]
             nxt, nxt2 = lam, nxt
-        fa_ref[n] = rs_in * nxt[:rows, :cols]
-        db = neg * (dd - 0.5 * du)
+        rs = pack[ITERS + 3]
+        fa_ref[n] = rs[:rows, :cols] * nxt[:rows, :cols]
+        db = -(rs * rs) * (dd - 0.5 * du)
         db_in = db[:rows, :cols]
-        ge_ref[n] = mre * eb + me * (db_in + east(db)[:rows, :cols])
-        gn_ref[n] = mrn * nb + mn * (db_in + north(db)[:rows, :cols])
+        ge_ref[n] = geo[2] * eb + geo[0] * (db_in + east(db)[:rows, :cols])
+        gn_ref[n] = geo[3] * nb + geo[1] * (db_in + north(db)[:rows, :cols])
+        for r in results(n):
+            r.start()
         return carry
 
     lax.fori_loop(0, costs, one, 0)
-    for c in copies + reduce_copies:
-        c.wait_send()
+    for n in range(costs):
+        for r in results(n):
+            r.wait()
 
 
 def solution(mesh):
@@ -334,12 +373,14 @@
             ref for g in stages for ref in (
                 pltpu.VMEM((1, 128), f32), pltpu.VMEM((len(g), 1, 128), f32),
                 dma((len(g),)), dma((len(g),)))]
-        vmem = pl.BlockSpec(memory_space=pltpu.VMEM)
-        return pl.pallas_call(
+        bf = rows + 2 * HB
+        shapes = ((costs, bf, ringc), (ITERS + 4, bf, ringc), (4, rows, cols), (3 * ITERS, costs, 128))
+        hbm = pl.BlockSpec(memory_space=pltpu.HBM)
+        mids = pl.pallas_call(
             functools.partial(kernel, nlat, nlon, stages),
-            out_shape=[jax.ShapeDtypeStruct((costs, rows, cols), f32)] * 3,
-            in_specs=[pl.BlockSpec(memory_space=pltpu.HBM)] * 6,
-            out_specs=[vmem] * 3,
+            out_shape=[jax.ShapeDtypeStruct(x, f32) for x in shapes],
+            in_specs=[hbm] * 6,
+            out_specs=[hbm] * 4,
             scratch_shapes=[
                 *[pltpu.VMEM((rows, cols), f32)] * 4,
                 pltpu.VMEM((rows, cols), jnp.int32),
@@ -356,8 +397,8 @@
                 pltpu.VMEM((costs, HB, cols), f32),
                 pltpu.VMEM((costs, HB, cols), f32),
                 pltpu.VMEM((nsum, 128), f32),
-                pltpu.VMEM((costs, rows + 2 * HB, ringc), f32),
-                pltpu.VMEM((3 * ITERS, costs, ringc), f32),
+                *[pltpu.VMEM(x, f32) for x in shapes],
+                dma((4,)),
                 dma((18,)),
                 dma((18,)),
                 *reduce_scratch,
@@ -366,6 +407,23 @@
                 collective_id=0, has_side_effects=True, vmem_limit_bytes=63 * 1024 * 1024
             ),
         )(forcing, depth_east, depth_north, surface_term, ocean_mask, cost_weights)
+        out = (costs, rows, cols)
+        return pl.pallas_call(
+            adjoint_kernel,
+            out_shape=[jax.ShapeDtypeStruct(out, f32)] * 3,
+            in_specs=[hbm] * 4,
+            out_specs=[hbm] * 3,
+            scratch_shapes=[
+                *[pltpu.VMEM(x, f32) for x in shapes],
+                *[pltpu.VMEM((ITERS, rows, cols), f32)] * 3,
+                pltpu.VMEM((ITERS + 1, bf, ringc), f32),
+                *[pltpu.VMEM(out, f32)] * 3,
+                dma((3,)),
+                dma((costs,)),
+                dma((3, costs)),
+            ],
+            compiler_params=pltpu.CompilerParams(vmem_limit_bytes=63 * 1024 * 1024),
+        )(*mids)
 
     grid = P("lat", "lon")
     field = P(None, "lat", "lon")

time: 34.5 us -> 32.6 us (0.945)
  local copies, waits for them, and re-layouts: 3.95 us -> 0 us
  Pallas kernels: 29.6 us -> 31.8 us
    pallas_call x0 -> x1, Pallas kernels: none -> 11.1 us  [body(): pl.pallas_call(adjoint_kernel, out_shape=[jax.ShapeDtypeStruct(out, f32)]...]
    pallas_call x1, Pallas kernels: 29.6 us -> 20.6 us  [body(): pl.pallas_call(functools.partial(kernel, nlat, nlon, stages), out_shape=[...]
    unnamed x7 -> x0, local copies, waits for them, and re-layouts: 3.95 us -> none
where the time goes in v3:
time: 32.6 us; the launch traced here: 32.4 us
  Pallas kernels  31.8 us (98%)
  between operations  0.64 us (2%)
    pallas_call x1, Pallas kernels, body(): pl.pallas_call(functools.partial(kernel, nlat, nlon, stages), out_shape=[...  20.6 us
    pallas_call x1, Pallas kernels, body(): pl.pallas_call(adjoint_kernel, out_shape=[jax.ShapeDtypeStruct(out, f32)]...  11.1 us

profile of v3, /device:TPU:0, one launch (start us, length us, event | category | flops | bytes accessed | tf_op | source)
XLA Modules:
  0.0 32.4 jit_solution(8180894592956052532)
XLA Ops:
  0.6 20.6 %shard_map.85 = (f32[8,80,384]{2,1,0:T(8,128)}, f32[10,80,384]{2,1,0:T(8,128)}, f32[4,64,256]{2,1,0:T(8,128)}, f32[18,8,128]{2,1,0:T(8,128)}) custom-call(f32[64,256]{1,0:T(8,128)} %f_hbm.1, f32[64,256]{1,0:T(8,128)} %de_hbm.1, f32[64,256]{1,0:T(8,128)} %dn_hbm.1, f32[64,256]{1,0:T(8,128)} %st_hbm.1, s32[64,256]{1,0:T(8,128)} %mk_hbm.1, f32[8,64,256]{2,1,0:T(8,128)} %w_hbm.1), custom_call_target="tpu_custom_call" | custom-call | tf_op jit(solution)/shard_map/pallas_call | solution.py:379
  21.3 11.1 %shard_map.86 = (f32[8,64,256]{2,1,0:T(8,128)}, f32[8,64,256]{2,1,0:T(8,128)}, f32[8,64,256]{2,1,0:T(8,128)}) custom-call(f32[8,80,384]{2,1,0:T(8,128)} %get-tuple-element.7.wp_hbm, f32[10,80,384]{2,1,0:T(8,128)} %get-tuple-element.8.pack_hbm, f32[4,64,256]{2,1,0:T(8,128)} %get-tuple-element.9.geo_hbm, f32[18,8,128]{2,1,0:T(8,128)} %get-tuple-element.10.coef_hbm), custom_call_target="tpu_custom_call" | custom-call | tf_op jit(solution)/shard_map/pallas_call | solution.py:411
